TPU v7x, 256 devices: a whole 4x4x8 slice. The times are simulated.
256 devices in a mesh: layer: 4 (over z_lo, core), feat: 64 (over y, z_hi, x).
Axes of the slice: x: 4, y: 4, z: 8 (z_hi: 4, z_lo: 2; z = z_hi * 2 + z_lo), core: 2. Of those that a mesh axis runs over, the one named last changes fastest.
Arguments:
- activations: bfloat16 [512, 4, 2304], P('feat', 'layer'), may hold values from -6 to 6
- enc_weight: bfloat16 [4, 2304, 65536], P('layer', None, 'feat'), may hold values from -0.0625 to 0.0625
- dec_weight: bfloat16 [4, 65536, 2304], P('layer', 'feat'), may hold values from -0.03125 to 0.03125
- enc_bias: float32 [65536], P('feat'), may hold values from -3 to 3
- threshold: float32 [65536], P('feat'), may hold values from 0.1 to 1
- dec_bias: float32 [4, 2304], P('layer'), may hold values from -3 to 3
- token_mask: int32 [512], replicated, may hold values 0 or 1
Outputs:
- squared_error: float32 [512, 4], P('feat', 'layer')
- latent_grad: float32 [512, 65536], P(None, 'feat')
- input_grad: bfloat16 [512, 4, 2304], P('feat', 'layer')
All inputs are finite; a program needn't handle non-finite values.
Results may differ from a plain program's by a relative error of at most 0.015.
Values may be sent and summed in bfloat16 or wider, within the bound.
A program may use at most 64 MiB of HBM per device.

v0:
```python
import jax
import jax.numpy as jnp
from jax import lax
from jax.sharding import Mesh
from jax.sharding import PartitionSpec as P

FEAT = ("feat_0", "feat_1", "feat_2")
jump_scale = 0.25


def split_up(array, dim, length):
    before, after = (array.shape[:dim], array.shape[dim + 1 :])
    return jnp.moveaxis(array.reshape(*before, length, -1, *after), dim, 0)


def sent_and_summed(array, axis, dim):
    length = lax.axis_size(axis)
    parts = lax.all_to_all(split_up(array, dim, length), axis, 0, 0, tiled=True)
    return jnp.sum(parts, axis=0)


def sum_by_axis(array, axes, dim):
    far, near = axes
    parts = split_up(array, dim, lax.axis_size(far))
    nearer = sent_and_summed(parts, near, dim + 1)
    arrived = lax.all_to_all(nearer, far, split_axis=0, concat_axis=0, tiled=True)
    return arrived.sum(axis=0)


def shards(activations, enc_weight, dec_weight, enc_bias, threshold, dec_bias, token_mask):
    tok_dev = activations.shape[0]
    partial_value = jnp.einsum(
        "tld,ldf->tf",
        lax.all_gather(activations, FEAT, axis=0, tiled=True),
        enc_weight,
        preferred_element_type=jnp.float32,
    )
    preact = lax.psum(partial_value.astype(jnp.bfloat16), "layer").astype(jnp.float32) + enc_bias
    gating = jax.nn.sigmoid((preact - threshold) / jump_scale)
    latent = (preact * gating).astype(jnp.bfloat16)
    gate_slope = gating + preact * gating * (1.0 - gating) / jump_scale
    first_row = lax.axis_index(FEAT) * tok_dev
    rows = latent
    rebuilt = sum_by_axis(
        jnp.einsum("tf,lfd->tld", rows, dec_weight, preferred_element_type=jnp.float32),
        (("feat_0", "feat_1"), "feat_2"),
        0,
    )
    own_mask = lax.dynamic_slice_in_dim(token_mask, first_row, tok_dev, 0).astype(jnp.float32)[
        :, None, None
    ]
    error = own_mask * (rebuilt + dec_bias[None, :, :] - activations.astype(jnp.float32))
    grad_part = jnp.einsum(
        "tld,lfd->tf",
        lax.all_gather(error.astype(jnp.bfloat16), FEAT, axis=0, tiled=True),
        dec_weight,
        preferred_element_type=jnp.float32,
    )
    squared_error = jnp.mean(error * error, axis=-1)
    latent_grad = lax.psum(grad_part.astype(jnp.bfloat16), "layer").astype(jnp.float32)
    preact_grad = (latent_grad * gate_slope).astype(jnp.bfloat16)
    rows = preact_grad
    grad_terms = sum_by_axis(
        jnp.einsum("tf,ldf->tld", rows, enc_weight, preferred_element_type=jnp.float32),
        (("feat_0", "feat_1"), "feat_2"),
        0,
    )
    input_grad = (grad_terms - error).astype(jnp.bfloat16)
    return (squared_error, latent_grad, input_grad)


def solution(mesh):
    finer = Mesh(
        mesh.devices.reshape(mesh.shape["layer"], 4, 4, 4), ("layer", "feat_0", "feat_1", "feat_2")
    )
    return jax.shard_map(
        shards,
        mesh=finer,
        in_specs=(
            P(FEAT, "layer", None),
            P("layer", None, FEAT),
            P("layer", FEAT, None),
            P(FEAT),
            P(FEAT),
            P("layer", None),
            P(),
        ),
        out_specs=(P(FEAT, "layer"), P(None, FEAT), P(FEAT, "layer", None)),
        check_vma=False,
    )
```

profile of v0, /device:TPU:32, one launch (start us, length us, event | category | flops | bytes accessed | tf_op | source)
XLA Modules:
  0.0 498.0 jit_solution(7002110068138016690)
XLA Ops:
  7.2 0.0 all-gather.3.cloned.1.call-start
  7.2 0.7 all-gather.3.cloned.1.call-update
  7.9 0.0 all-reduce.3.cloned.1.call-start
  8.0 84.0 %all-gather.3.cloned.1.call-done = bf16[512,1,2304]{2,0,1:T(8,128)(2,1)} async-done(((bf16[8,1,2304]{2,0,1:T(8,128)(2,1)}), bf16[512,1,2304]{2,0,1:T(8,128)(2,1)}) %all-gather.3.cloned.1.call-update) | async-done | bytes 2359312 | tf_op jit(solution)/shard_map/all_gather | solution.py:34
  91.9 6.6 %fusion.10 = bf16[512,1024]{1,0:T(8,128)(2,1)} fusion(bf16[1,2304,1024]{2,1,0:T(8,128)(2,1)} %param.8, bf16[512,1,2304]{2,0,1:T(8,128)(2,1)} %all-gather.3.cloned.1.call-done), kind=kOutput, calls=%fused_computation.15 | convolution fusion | flops 2416443392 | bytes 8126464 | tf_op jit(solution)/shard_map/tld,ldf->tf/dot_general | solution.py:32
  98.6 0.0 all-reduce.3.cloned.1.call-update
  98.6 44.8 %all-reduce.3.cloned.1.call-done = bf16[512,1024]{1,0:T(8,128)(2,1)} async-done(((bf16[512,1024]{1,0:T(8,128)(2,1)}), bf16[512,1024]{1,0:T(8,128)(2,1)}) %all-reduce.3.cloned.1.call-update) | async-done | bytes 1048592 | tf_op jit(solution)/shard_map/psum | solution.py:38
  143.4 1.9 fusion.9
  145.3 4.9 convolution_bitcast_fusion.1
  150.2 0.4 copy.10
  150.6 58.9 %all_to_all.20 = f32[4,16,8,1,2304]{4,2,1,3,0:T(8,128)} all-to-all(f32[4,16,8,1,2304]{4,2,1,3,0:T(8,128)S(1)} %copy.10), channel_id=1, replica_groups=mesh['layer'=4,'feat_0'=4,'feat_1'=4,'feat_2'=4] {'feat_2'}, dimensions={0} | all-to-all | bytes 9437184 | tf_op jit(solution)/shard_map/all_to_all | solution.py:18
  209.6 3.7 reduce_sum.53
  213.3 9.2 %all-to-all-start.1 = ((f32[16,8,1,2304]{3,1,2,0:T(8,128)}), f32[16,8,1,2304]{3,1,2,0:T(8,128)S(1)}, u32[]{:S(2)}, u32[]{:S(2)}) async-start(f32[16,8,1,2304]{3,1,2,0:T(8,128)} %bitcast.8), calls=%async_computation.1 | async-start | bytes 2359296 | tf_op jit(solution)/shard_map/all_to_all | solution.py:26
  222.5 0.0 all-gather.5.cloned.1.call-start
  222.6 0.8 dynamic-slice_convert_fusion
  223.4 31.0 %all-to-all-done.1 = f32[16,8,1,2304]{3,1,2,0:T(8,128)S(1)} async-done(((f32[16,8,1,2304]{3,1,2,0:T(8,128)}), f32[16,8,1,2304]{3,1,2,0:T(8,128)S(1)}, u32[]{:S(2)}, u32[]{:S(2)}) %all-to-all-start.1) | async-done | bytes 1179680 | tf_op jit(solution)/shard_map/all_to_all | solution.py:26
  254.4 0.1 reduce_sum.55
  254.5 0.7 fusion.23
  255.2 0.0 all-gather.5.cloned.1.call-update
  255.2 0.2 all-reduce.5.cloned.1.call-start
  255.5 71.8 %all-gather.5.cloned.1.call-done = bf16[512,1,2304]{2,0,1:T(8,128)(2,1)} async-done(((bf16[8,1,2304]{2,0,1:T(8,128)(2,1)}), bf16[512,1,2304]{2,0,1:T(8,128)(2,1)}) %all-gather.5.cloned.1.call-update) | async-done | bytes 2359312 | tf_op jit(solution)/shard_map/all_gather | solution.py:55
  327.3 6.7 %fusion.15 = bf16[512,1024]{1,0:T(8,128)(2,1)} fusion(bf16[1,1024,2304]{2,1,0:T(8,128)(2,1)} %param.9, bf16[512,1,2304]{2,0,1:T(8,128)(2,1)} %all-gather.5.cloned.1.call-done), kind=kOutput, calls=%fused_computation.16 | convolution fusion | flops 2416443392 | bytes 8126464 | tf_op jit(solution)/shard_map/tld,lfd->tf/dot_general | solution.py:53
  333.9 44.7 %all-reduce.5.cloned.1.call-done = bf16[512,1024]{1,0:T(8,128)(2,1)} async-done(((bf16[512,1024]{1,0:T(8,128)(2,1)}), bf16[512,1024]{1,0:T(8,128)(2,1)}) %all-reduce.5.cloned.1.call-update) | async-done | bytes 1048592 | tf_op jit(solution)/shard_map/psum | solution.py:60
  378.7 3.6 multiply_convert_fusion
  382.3 5.0 %convolution_bitcast_fusion = f32[4,16,8,1,2304]{4,2,0,1,3:T(8,128)S(1)} fusion(bf16[16,4,8,1024]{3,2,1,0:T(8,128)(2,1)S(1)} %bitcast.65, bf16[1,2304,1024]{2,1,0:T(8,128)(2,1)} %param.8), kind=kOutput, calls=%fused_computation | convolution fusion | flops 2415919104 | bytes 10485760 | tf_op jit(solution)/shard_map/tf,ldf->tld/dot_general | solution.py:64
  387.3 0.4 copy.11
  387.7 58.9 %all_to_all.21 = f32[4,16,8,1,2304]{4,2,1,3,0:T(8,128)} all-to-all(f32[4,16,8,1,2304]{4,2,1,3,0:T(8,128)S(1)} %copy.11), channel_id=1, replica_groups=mesh['layer'=4,'feat_0'=4,'feat_1'=4,'feat_2'=4] {'feat_2'}, dimensions={0} | all-to-all | bytes 9437184 | tf_op jit(solution)/shard_map/all_to_all | solution.py:18
  446.6 2.7 reduce_sum.58
  449.4 40.7 %all_to_all.22 = f32[16,8,1,2304]{3,1,2,0:T(8,128)S(1)} all-to-all(f32[16,8,1,2304]{3,1,2,0:T(8,128)S(1)} %bitcast.64), channel_id=1, replica_groups=mesh['layer'=4,'feat_0'=4,'feat_1'=4,'feat_2'=4] {'feat_0','feat_1'}, dimensions={0} | all-to-all | bytes 2359296 | tf_op jit(solution)/shard_map/all_to_all | solution.py:26
  490.1 0.1 reduce_sum.60
  490.1 0.8 fusion.20
  490.9 0.5 multiply_bitcast_fusion
  (12 shorter events, 0.1 us)
Async XLA Ops:
  7.2 84.8 %all-gather.3.cloned.1.call-start = ((), (), s32[]{:S(2)}) async-start(), calls=%async_computation.4 | async-start | bytes 2396160 | tf_op jit(solution)/shard_map/all_gather | solution.py:34
  7.9 135.5 %copy-start.2 = (f32[1024]{0:T(1024)S(1)}, f32[1024]{0:T(1024)}, u32[]{:S(2)}) copy-start(f32[1024]{0:T(1024)} %param.11) | copy-start | bytes 12292
  7.9 135.5 %copy-start.3 = (f32[1024]{0:T(1024)S(1)}, f32[1024]{0:T(1024)}, u32[]{:S(2)}) copy-start(f32[1024]{0:T(1024)} %param.10) | copy-start | bytes 12292
  7.9 135.4 %all-reduce.3.cloned.1.call-start = ((), (), s32[]{:S(2)}) async-start(), calls=%async_computation.5 | async-start | bytes 2097152 | tf_op jit(solution)/shard_map/psum | solution.py:38
  213.3 9.3 %copy-start.4 = (f32[1,2304]{1,0:T(1,128)S(1)}, f32[1,2304]{1,0:T(1,128)}, u32[]{:S(2)}) copy-start(f32[1,2304]{1,0:T(1,128)} %param.12) | copy-start | bytes 27652
  213.3 41.2 %copy-start.1 = (bf16[8,1,2304]{2,0,1:T(8,128)(2,1)S(1)}, bf16[8,1,2304]{2,0,1:T(8,128)(2,1)}, u32[]{:S(2)}) copy-start(bf16[8,1,2304]{2,0,1:T(8,128)(2,1)} %param.7) | copy-start | bytes 110596
  213.3 41.1 %all-to-all-start.1 = ((f32[16,8,1,2304]{3,1,2,0:T(8,128)}), f32[16,8,1,2304]{3,1,2,0:T(8,128)S(1)}, u32[]{:S(2)}, u32[]{:S(2)}) async-start(f32[16,8,1,2304]{3,1,2,0:T(8,128)} %bitcast.8), calls=%async_computation.1 | async-start | bytes 2359296 | tf_op jit(solution)/shard_map/all_to_all | solution.py:26
  222.5 104.7 %all-gather.5.cloned.1.call-start = ((), (), s32[]{:S(2)}) async-start(), calls=%async_computation.6 | async-start | bytes 2396160 | tf_op jit(solution)/shard_map/all_gather | solution.py:55
  255.2 123.4 %copy-start = (bf16[512,1024]{1,0:T(8,128)(2,1)S(1)}, bf16[512,1024]{1,0:T(8,128)(2,1)}, u32[]{:S(2)}) copy-start(bf16[512,1024]{1,0:T(8,128)(2,1)} %all-reduce.3.cloned.1.call-done) | copy-start | bytes 3145732
  255.2 123.4 %all-reduce.5.cloned.1.call-start = ((), (), s32[]{:S(2)}) async-start(), calls=%async_computation.7 | async-start | bytes 2097152 | tf_op jit(solution)/shard_map/psum | solution.py:60
Sparse Core Ops, SparseCore 0:
  11.2 80.7 all-gather.2
  98.7 44.6 all-reduce.2
  255.3 71.8 all-gather.4
  334.1 44.5 all-reduce.4
where the time goes:
time: 499 us; the launch traced here: 498 us
  waiting for transfers between devices  277 us (56%)
  blocking collectives  159 us (32%)
  matrix products  23.2 us (5%)
  other arithmetic  14.9 us (3%)
  between operations  13.9 us (3%)
  starting transfers between devices  9.54 us (2%)
    all_to_all x2, blocking collectives, sent_and_summed(): parts = lax.all_to_all(split_up(array, dim, length), axis, 0, 0, tiled=True)  118 us
    all_gather x1, waiting for transfers between devices, shards(): lax.all_gather(activations, FEAT, axis=0, tiled=True)  84 us
    all_gather x1, waiting for transfers between devices, shards(): lax.all_gather(error.astype(jnp.bfloat16), FEAT, axis=0, tiled=True)  71.8 us
    psum x1, waiting for transfers between devices, shards(): lax.psum(partial_value.astype(jnp.bfloat16), 'layer').astype(jnp.float32)  44.8 us
    psum x1, waiting for transfers between devices, shards(): lax.psum(grad_part.astype(jnp.bfloat16), 'layer').astype(jnp.float32)  44.7 us
    all_to_all x1, blocking collectives, sum_by_axis(): lax.all_to_all(nearer, far, split_axis=0, concat_axis=0, tiled=True)  40.7 us
    all_to_all x1, waiting for transfers between devices, sum_by_axis(): lax.all_to_all(nearer, far, split_axis=0, concat_axis=0, tiled=True)  31 us
  transfers between devices with their start and end apart: 5, of which 5 were waited for; matrix products, arithmetic and copies ran while one was open for 0% of the time, Pallas kernels for 0%

commit v1 on v0

--- a/solution.py
+++ b/solution.py
@@ -6,6 +6,11 @@
 
 FEAT = ("feat_0", "feat_1", "feat_2")
 jump_scale = 0.25
+
+
+def exchange_gather(x, name, dim):
+    sent = jnp.stack([x] * lax.axis_size(name))
+    return jnp.concatenate(lax.all_to_all(sent, name, 0, 0), axis=dim)
 
 
 def split_up(array, dim, length):
@@ -31,7 +36,7 @@
     tok_dev = activations.shape[0]
     partial_value = jnp.einsum(
         "tld,ldf->tf",
-        lax.all_gather(activations, FEAT, axis=0, tiled=True),
+        exchange_gather(activations, FEAT, 0),
         enc_weight,
         preferred_element_type=jnp.float32,
     )

time: 499 us -> 480 us (0.962)
  waiting for transfers between devices: 277 us -> 188 us
  blocking collectives: 159 us -> 231 us
    all_gather x1 -> x0, waiting for transfers between devices: 84 us -> none  [shards(): lax.all_gather(activations, FEAT, axis=0, tiled=True)]
    all_to_all x0 -> x1, blocking collectives: none -> 72.8 us  [exchange_gather(): return jnp.concatenate(lax.all_to_all(sent, name, 0, 0), axis=dim)]
  transfers between devices with their start and end apart: 5 -> 4, of which waited for: 5 -> 4; matrix products, arithmetic and copies ran while one was open for 0% -> 0% of each run, Pallas kernels for 0% -> 0%
where the time goes in v1:
time: 480 us
  blocking collectives  231 us (48%)
  waiting for transfers between devices  188 us (39%)
  matrix products  20.2 us (4%)
  other arithmetic  14.9 us (3%)
  between operations  13.8 us (3%)
  starting transfers between devices  9.5 us (2%)
    all_to_all x2, blocking collectives, sent_and_summed(): parts = lax.all_to_all(split_up(array, dim, length), axis, 0, 0, tiled=True)  118 us
    all_to_all x1, blocking collectives, exchange_gather(): return jnp.concatenate(lax.all_to_all(sent, name, 0, 0), axis=dim)  72.8 us
    all_gather x1, waiting for transfers between devices, shards(): lax.all_gather(error.astype(jnp.bfloat16), FEAT, axis=0, tiled=True)  71.8 us
    psum x1, waiting for transfers between devices, shards(): lax.psum(grad_part.astype(jnp.bfloat16), 'layer').astype(jnp.float32)  44.8 us
    all_to_all x1, blocking collectives, sum_by_axis(): lax.all_to_all(nearer, far, split_axis=0, concat_axis=0, tiled=True)  40.7 us
    psum x1, waiting for transfers between devices, shards(): lax.psum(partial_value.astype(jnp.bfloat16), 'layer').astype(jnp.float32)  40.5 us
    all_to_all x1, waiting for transfers between devices, sum_by_axis(): lax.all_to_all(nearer, far, split_axis=0, concat_axis=0, tiled=True)  31 us
  transfers between devices with their start and end apart: 4, of which 4 were waited for; matrix products, arithmetic and copies ran while one was open for 0% of the time, Pallas kernels for 0%

profile of v1, /device:TPU:32, one launch (start us, length us, event | category | flops | bytes accessed | tf_op | source)
XLA Modules:
  0.0 479.7 jit_solution(17481629215664455904)
XLA Ops:
  7.2 0.0 all-reduce.3.cloned.1.call-start
  7.2 0.9 stack.2
  8.1 72.8 %all_to_all.25 = bf16[64,8,1,2304]{3,1,2,0:T(8,128)(2,1)S(1)} all-to-all(bf16[64,8,1,2304]{3,1,2,0:T(8,128)(2,1)S(1)} %stack.2), channel_id=1, replica_groups=mesh['layer'=4,'feat_0'=4,'feat_1'=4,'feat_2'=4] {'feat_0','feat_1','fea..., dimensions={0} | all-to-all | bytes 4718592 | tf_op jit(solution)/shard_map/all_to_all | solution.py:13
  81.0 3.6 fusion.10
  84.5 0.0 all-reduce.3.cloned.1.call-update
  84.5 40.5 %all-reduce.3.cloned.1.call-done = bf16[512,1024]{1,0:T(8,128)(2,1)} async-done(((bf16[512,1024]{1,0:T(8,128)(2,1)}), bf16[512,1024]{1,0:T(8,128)(2,1)}) %all-reduce.3.cloned.1.call-update) | async-done | bytes 1048592 | tf_op jit(solution)/shard_map/psum | solution.py:43
  125.0 1.9 fusion.9
  126.9 4.9 %convolution_bitcast_fusion.1 = f32[4,16,8,1,2304]{4,2,0,1,3:T(8,128)S(1)} fusion(bf16[16,4,8,1024]{3,2,1,0:T(8,128)(2,1)S(1)} %bitcast.67, bf16[1,1024,2304]{2,1,0:T(8,128)(2,1)} %param.9), kind=kOutput, calls=%fused_computation.1 | convolution fusion | flops 2415919104 | bytes 10485760 | tf_op jit(solution)/shard_map/tf,lfd->tld/dot_general | solution.py:50
  131.8 0.4 copy.10
  132.3 58.9 %all_to_all.26 = f32[4,16,8,1,2304]{4,2,1,3,0:T(8,128)} all-to-all(f32[4,16,8,1,2304]{4,2,1,3,0:T(8,128)S(1)} %copy.10), channel_id=1, replica_groups=mesh['layer'=4,'feat_0'=4,'feat_1'=4,'feat_2'=4] {'feat_2'}, dimensions={0} | all-to-all | bytes 9437184 | tf_op jit(solution)/shard_map/all_to_all | solution.py:23
  191.2 3.7 reduce_sum.53
  195.0 9.2 %all-to-all-start.2 = ((f32[16,8,1,2304]{3,1,2,0:T(8,128)}), f32[16,8,1,2304]{3,1,2,0:T(8,128)S(1)}, u32[]{:S(2)}, u32[]{:S(2)}) async-start(f32[16,8,1,2304]{3,1,2,0:T(8,128)} %bitcast.9), calls=%async_computation.2 | async-start | bytes 2359296 | tf_op jit(solution)/shard_map/all_to_all | solution.py:31
  204.2 0.0 all-gather.2.cloned.1.call-start
  204.3 0.8 dynamic-slice_convert_fusion
  205.0 31.0 %all-to-all-done.2 = f32[16,8,1,2304]{3,1,2,0:T(8,128)S(1)} async-done(((f32[16,8,1,2304]{3,1,2,0:T(8,128)}), f32[16,8,1,2304]{3,1,2,0:T(8,128)S(1)}, u32[]{:S(2)}, u32[]{:S(2)}) %all-to-all-start.2) | async-done | bytes 1179680 | tf_op jit(solution)/shard_map/all_to_all | solution.py:31
  236.1 0.1 reduce_sum.55
  236.1 0.7 fusion.23
  236.8 0.0 all-gather.2.cloned.1.call-update
  236.9 0.2 all-reduce.5.cloned.1.call-start
  237.1 71.8 %all-gather.2.cloned.1.call-done = bf16[512,1,2304]{2,0,1:T(8,128)(2,1)} async-done(((bf16[8,1,2304]{2,0,1:T(8,128)(2,1)}), bf16[512,1,2304]{2,0,1:T(8,128)(2,1)}) %all-gather.2.cloned.1.call-update) | async-done | bytes 2359312 | tf_op jit(solution)/shard_map/all_gather | solution.py:60
  308.9 6.7 %fusion.15 = bf16[512,1024]{1,0:T(8,128)(2,1)} fusion(bf16[1,1024,2304]{2,1,0:T(8,128)(2,1)} %param.9, bf16[512,1,2304]{2,0,1:T(8,128)(2,1)} %all-gather.2.cloned.1.call-done), kind=kOutput, calls=%fused_computation.16 | convolution fusion | flops 2416443392 | bytes 8126464 | tf_op jit(solution)/shard_map/tld,lfd->tf/dot_general | solution.py:58
  315.6 0.0 all-reduce.5.cloned.1.call-update
  315.6 44.8 %all-reduce.5.cloned.1.call-done = bf16[512,1024]{1,0:T(8,128)(2,1)} async-done(((bf16[512,1024]{1,0:T(8,128)(2,1)}), bf16[512,1024]{1,0:T(8,128)(2,1)}) %all-reduce.5.cloned.1.call-update) | async-done | bytes 1048592 | tf_op jit(solution)/shard_map/psum | solution.py:65
  360.3 3.6 multiply_convert_fusion
  364.0 5.0 %convolution_bitcast_fusion = f32[4,16,8,1,2304]{4,2,0,1,3:T(8,128)S(1)} fusion(bf16[16,4,8,1024]{3,2,1,0:T(8,128)(2,1)S(1)} %bitcast.66, bf16[1,2304,1024]{2,1,0:T(8,128)(2,1)} %param.8), kind=kOutput, calls=%fused_computation | convolution fusion | flops 2415919104 | bytes 10485760 | tf_op jit(solution)/shard_map/tf,ldf->tld/dot_general | solution.py:69
  369.0 0.4 copy.11
  369.4 58.9 %all_to_all.27 = f32[4,16,8,1,2304]{4,2,1,3,0:T(8,128)} all-to-all(f32[4,16,8,1,2304]{4,2,1,3,0:T(8,128)S(1)} %copy.11), channel_id=1, replica_groups=mesh['layer'=4,'feat_0'=4,'feat_1'=4,'feat_2'=4] {'feat_2'}, dimensions={0} | all-to-all | bytes 9437184 | tf_op jit(solution)/shard_map/all_to_all | solution.py:23
  428.3 2.7 reduce_sum.58
  431.0 40.7 %all_to_all.28 = f32[16,8,1,2304]{3,1,2,0:T(8,128)S(1)} all-to-all(f32[16,8,1,2304]{3,1,2,0:T(8,128)S(1)} %bitcast.65), channel_id=1, replica_groups=mesh['layer'=4,'feat_0'=4,'feat_1'=4,'feat_2'=4] {'feat_0','feat_1'}, dimensions={0} | all-to-all | bytes 2359296 | tf_op jit(solution)/shard_map/all_to_all | solution.py:31
  471.7 0.1 reduce_sum.60
  471.8 0.8 fusion.20
  472.6 0.5 multiply_bitcast_fusion
  (13 shorter events, 0.1 us)
Async XLA Ops:
  7.2 117.8 %all-reduce.3.cloned.1.call-start = ((), (), s32[]{:S(2)}) async-start(), calls=%async_computation.5 | async-start | bytes 2097152 | tf_op jit(solution)/shard_map/psum | solution.py:43
  8.1 72.8 %copy-start.5 = (bf16[1,2304,1024]{2,1,0:T(8,128)(2,1)S(1)}, bf16[1,2304,1024]{2,1,0:T(8,128)(2,1)}, u32[]{:S(2)}) copy-start(bf16[1,2304,1024]{2,1,0:T(8,128)(2,1)} %param.8) | copy-start | bytes 14155780
  80.9 44.1 %copy-start.2 = (f32[1024]{0:T(1024)S(1)}, f32[1024]{0:T(1024)}, u32[]{:S(2)}) copy-start(f32[1024]{0:T(1024)} %param.11) | copy-start | bytes 12292
  80.9 44.1 %copy-start.3 = (f32[1024]{0:T(1024)S(1)}, f32[1024]{0:T(1024)}, u32[]{:S(2)}) copy-start(f32[1024]{0:T(1024)} %param.10) | copy-start | bytes 12292
  194.9 9.3 %copy-start.4 = (f32[1,2304]{1,0:T(1,128)S(1)}, f32[1,2304]{1,0:T(1,128)}, u32[]{:S(2)}) copy-start(f32[1,2304]{1,0:T(1,128)} %param.12) | copy-start | bytes 27652
  195.0 41.2 %copy-start.1 = (bf16[8,1,2304]{2,0,1:T(8,128)(2,1)S(1)}, bf16[8,1,2304]{2,0,1:T(8,128)(2,1)}, u32[]{:S(2)}) copy-start(bf16[8,1,2304]{2,0,1:T(8,128)(2,1)} %param.7) | copy-start | bytes 110596
  195.0 41.1 %all-to-all-start.2 = ((f32[16,8,1,2304]{3,1,2,0:T(8,128)}), f32[16,8,1,2304]{3,1,2,0:T(8,128)S(1)}, u32[]{:S(2)}, u32[]{:S(2)}) async-start(f32[16,8,1,2304]{3,1,2,0:T(8,128)} %bitcast.9), calls=%async_computation.2 | async-start | bytes 2359296 | tf_op jit(solution)/shard_map/all_to_all | solution.py:31
  204.2 104.7 %all-gather.2.cloned.1.call-start = ((), (), s32[]{:S(2)}) async-start(), calls=%async_computation.6 | async-start | bytes 2396160 | tf_op jit(solution)/shard_map/all_gather | solution.py:60
  236.9 123.5 %copy-start = (bf16[512,1024]{1,0:T(8,128)(2,1)S(1)}, bf16[512,1024]{1,0:T(8,128)(2,1)}, u32[]{:S(2)}) copy-start(bf16[512,1024]{1,0:T(8,128)(2,1)} %all-reduce.3.cloned.1.call-done) | copy-start | bytes 3145732
  236.9 123.5 %all-reduce.5.cloned.1.call-start = ((), (), s32[]{:S(2)}) async-start(), calls=%async_computation.7 | async-start | bytes 2097152 | tf_op jit(solution)/shard_map/psum | solution.py:65
Sparse Core Ops, SparseCore 0:
  84.7 40.2 all-reduce.2
  237.0 71.8 all-gather.1
  315.7 44.6 all-reduce.4
